TPU v7x, 256 devices: a whole 4x4x8 slice. The times are simulated.
256 devices in a mesh: epoch: 16 (over y, x), blend: 16 (over z, core).
Axes of the slice: x: 4, y: 4, z: 8, core: 2. Of those that a mesh axis runs over, the one named last changes fastest.
Arguments:
- visit_flux: bfloat16 [64, 64, 6, 16384], P('epoch', None, None, 'blend'), may hold values from -6 to 6
- visit_precision: bfloat16 [64, 64, 6, 16384], P('epoch', None, None, 'blend'), may hold values from 0.25 to 4
- visit_live: int32 [64, 64], P('epoch'), may hold values 0 or 1
- footprint: int32 [64, 8, 16384], P('blend', None, 'epoch'), may hold values 0 or 1
- source_count: int32 [64], P('blend'), may hold values from 1 to 8
- spectra_init: float32 [64, 8, 6], P('blend'), may hold values from 0.2 to 1.2
- morphology_init: float32 [64, 8, 16384], P('blend', None, 'epoch'), may hold values from 0 to 0.25
Outputs:
- coadd_flux: float32 [64, 6, 16384], P('blend', None, 'epoch')
- spectra: float32 [64, 8, 6], P('blend')
- morphology: float32 [64, 8, 16384], P('blend', None, 'epoch')
All inputs are finite; a program needn't handle non-finite values. No bound on the sum of `visit_live` or of `footprint` on one device may be relied on, other than what follows from the above.
Results may differ from a plain program's by a relative error of at most 0.0003.
Values sent between devices are 32-bit elements; how exact they have to be, the bound alone decides.
No kernel may reach another device: no remote copies, remote signals or barrier semaphores. Data moves between devices by JAX's collectives and lax.ppermute only.
A program may use at most 64 MiB of HBM per device.

v0:
```python
import jax
import jax.numpy as jnp
from jax import lax
from jax.sharding import PartitionSpec as P

ITERS = 2


def in_blocks(array, dim, count):
    shape = array.shape
    pieces = array.reshape(*shape[:dim], count, shape[dim] // count, *shape[dim + 1 :])
    return jnp.moveaxis(pieces, dim, 0)


def sent_and_summed(array, axis, dim):
    pieces = in_blocks(array, dim, lax.axis_size(axis))
    arrived = lax.all_to_all(pieces, axis, split_axis=0, concat_axis=0, tiled=True)
    return arrived.sum(axis=0)


def side_by_side(arrays, axis, dim, along):
    widths = [a.shape[along] for a in arrays]
    both = jnp.concatenate(arrays, axis=along)
    filled = sent_and_summed(both, axis, dim)
    return tuple(jnp.split(filled, [sum(widths[:k]) for k in range(1, len(widths))], axis=along))


def side_by_side_2(arrays, axis, split_dim, concat_dim, along):
    widths = [a.shape[along] for a in arrays]
    both = jnp.concatenate(arrays, axis=along)
    filled = lax.all_to_all(both, axis, split_axis=split_dim, concat_axis=concat_dim, tiled=True)
    return tuple(jnp.split(filled, [sum(widths[:k]) for k in range(1, len(widths))], axis=along))


def from_everyone(array, axis):
    copies = jnp.broadcast_to(array, (lax.axis_size(axis), *array.shape))
    return lax.all_to_all(copies, axis, split_axis=0, concat_axis=0, tiled=True)


def of_everyone(array, axis):
    return from_everyone(array, axis).sum(axis=0)


def together(arrays, axis):
    line, at, finished = (jnp.concatenate([a.reshape(-1) for a in arrays]), 0, [])
    subtotal = of_everyone(line, axis)
    for a in arrays:
        finished.append(subtotal[at : at + a.size].reshape(a.shape))
        at += a.size
    return tuple(finished)


def on_device(
    visit_flux, visit_precision, visit_live, footprint, source_count, spectra_init, morphology_init
):
    weights = visit_precision.astype(jnp.float32) * visit_live.astype(jnp.float32)[:, :, None, None]
    numerator = jnp.sum(weights * visit_flux.astype(jnp.float32), axis=0)
    weight_sum = jnp.sum(weights, axis=0)
    pix_part = morphology_init.shape[2]
    owned = morphology_init.shape[0]
    numerator, weight_sum = side_by_side((numerator, weight_sum), "epoch", 2, 0)
    every_blend, band_count, piece = numerator.shape
    numerator = numerator.reshape(every_blend, band_count, 1, piece)
    weight_sum = weight_sum.reshape(every_blend, band_count, 1, piece)
    numerator, weight_sum = side_by_side_2((numerator, weight_sum), "blend", 0, 2, 1)
    blocks = numerator.shape[2]
    numerator = numerator.reshape(owned, band_count, blocks, 1, piece)
    weight_sum = weight_sum.reshape(owned, band_count, blocks, 1, piece)
    numerator, weight_sum = side_by_side_2((numerator, weight_sum), "epoch", 2, 3, 0)
    numerator = numerator.reshape(owned, band_count, pix_part)
    weight_sum = weight_sum.reshape(owned, band_count, pix_part)
    coadd_flux = numerator / (1.0 + weight_sum)
    coverage = weight_sum / (1.0 + weight_sum)
    slots = footprint.shape[1]
    source_live = (jnp.arange(slots, dtype=jnp.int32)[None, :] < source_count[:, None]).astype(
        jnp.float32
    )
    footprint_mask = footprint.astype(jnp.float32) * source_live[:, :, None]
    live_count = source_count.astype(jnp.float32)
    morphology = morphology_init * footprint_mask
    spectra = spectra_init
    highest = lax.Precision.HIGHEST
    for iteration in range(ITERS):
        blend_model = jnp.einsum("bkc,bkp->bcp", spectra, morphology, precision=highest)
        residual = coverage * (coadd_flux - blend_model)
        morph_grad = jnp.einsum("bkc,bcp->bkp", spectra, residual, precision=highest)
        morph_step = 1.0 / (1.0 + live_count[:, None] * jnp.sum(spectra * spectra, axis=2))
        morphology = (
            jnp.maximum(0.0, morphology + morph_grad * morph_step[:, :, None]) * footprint_mask
        )
        blend_model = jnp.einsum("bkc,bkp->bcp", spectra, morphology, precision=highest)
        residual = coverage * (coadd_flux - blend_model)
        spectra_grad = jnp.einsum("bkp,bcp->bkc", morphology, residual, precision=highest)
        morph_norm = jnp.sum(morphology * morphology, axis=2)
        spectra_grad, morph_norm = together((spectra_grad, morph_norm), "epoch")
        spectra = jnp.maximum(
            0.0, spectra + spectra_grad / (1.0 + live_count[:, None] * morph_norm)[:, :, None]
        )
    return (coadd_flux, spectra, morphology)


def solution(mesh):
    in_specs = (
        P("epoch", None, None, "blend"),
        P("epoch", None, None, "blend"),
        P("epoch", None),
        P("blend", None, "epoch"),
        P("blend"),
        P("blend", None, None),
        P("blend", None, "epoch"),
    )
    out_specs = (P("blend", None, "epoch"), P("blend", None, None), P("blend", None, "epoch"))
    return jax.shard_map(
        on_device, mesh=mesh, in_specs=in_specs, out_specs=out_specs, check_vma=False
    )
```

profile of v0, /device:TPU:2, one launch (start us, length us, event | category | flops | bytes accessed | tf_op | source)
XLA Modules:
  0.0 122.1 jit_solution(499427961824183499)
XLA Ops:
  0.6 0.7 convert_element_type.23
  1.3 5.1 %multiply_reduce_fusion = (f32[64,6,1024]{2,0,1:T(8,128)S(1)}, f32[64,6,1024]{2,0,1:T(8,128)S(1)}) fusion(bf16[4,64,6,1024]{3,1,2,0:T(8,128)(2,1)} %param.7, bf16[4,64,6,1024]{3,1,2,0:T(8,128)(2,1)} %param.8, f32[4,64]{1,0:T(4,128)S(1)} %convert_element_type.23), kind=kLoop, calls=%fused_computation | loop fusion | flops 8650752 | bytes 9438208 | tf_op jit(solution)/shard_map/reduce_sum | solution.py:57
  6.4 0.2 pad_maximum_fusion
  6.6 2.4 %copy.93 = f32[128,6,1024]{0,2,1:T(8,128)} copy(f32[128,6,1024]{2,0,1:T(8,128)S(1)} %pad_maximum_fusion) | data formatting | bytes 6291456 | tf_op jit(solution)/shard_map/concatenate | solution.py:23
  9.0 2.1 %copy.94 = f32[16,128,6,64]{1,3,2,0:T(8,128)S(1)} copy(f32[16,128,6,64]{1,3,0,2:T(8,128)} %bitcast.62) | data formatting | bytes 6291456 | tf_op jit(solution)/shard_map/transpose | solution.py:12
  11.1 45.5 %all_to_all.44 = f32[16,128,6,64]{1,3,2,0:T(8,128)S(1)} all-to-all(f32[16,128,6,64]{1,3,2,0:T(8,128)S(1)} %copy.94), channel_id=1, replica_groups=mesh['epoch'=16,'blend'=16] {'epoch'}, dimensions={0} | all-to-all | bytes 6291456 | tf_op jit(solution)/shard_map/all_to_all | solution.py:17
  56.7 0.2 reduce_sum.83
  56.9 0.1 slice_bitcast_fusion.3
  57.0 0.5 broadcast.129
  57.5 0.7 reduce.2
  58.2 0.3 copy.134
  58.5 0.9 reshape.200
  59.4 8.6 %all-to-all-start.1 = ((f32[16,1,3072]{2,1,0:T(1,128)}), f32[16,1,3072]{2,1,0:T(1,128)S(1)}, u32[]{:S(2)}, u32[]{:S(2)}) async-start(f32[16,1,3072]{2,1,0:T(1,128)} %reshape.200), calls=%async_computation.1 | async-start | bytes 393216 | tf_op jit(solution)/shard_map/all_to_all | solution.py:31
  68.0 0.0 copy-done.4
  68.0 0.0 copy-done.3
  68.0 0.1 copy.108
  68.2 0.1 add_divide_fusion.3
  68.2 9.7 %all-to-all-done.1 = f32[16,1,3072]{2,1,0:T(1,128)S(1)} async-done(((f32[16,1,3072]{2,1,0:T(1,128)}), f32[16,1,3072]{2,1,0:T(1,128)S(1)}, u32[]{:S(2)}, u32[]{:S(2)}) %all-to-all-start.1) | async-done | bytes 196640 | tf_op jit(solution)/shard_map/all_to_all | solution.py:31
  77.9 1.1 reduce.3
  79.0 0.5 reshape.201
  79.5 0.0 copy-start.1
  79.5 0.0 copy-start.2
  79.6 0.1 copy_bitcast_fusion
  79.7 0.9 reshape.202
  80.6 4.8 %all-to-all-start.2 = ((f32[16,1,3072]{2,1,0:T(1,128)}), f32[16,1,3072]{2,1,0:T(1,128)S(1)}, u32[]{:S(2)}, u32[]{:S(2)}) async-start(f32[16,1,3072]{2,1,0:T(1,128)} %reshape.202), calls=%async_computation.2 | async-start | bytes 393216 | tf_op jit(solution)/shard_map/all_to_all | solution.py:31
  85.4 0.1 fusion.19
  85.4 7.8 %all-to-all-done.2 = f32[16,1,3072]{2,1,0:T(1,128)S(1)} async-done(((f32[16,1,3072]{2,1,0:T(1,128)}), f32[16,1,3072]{2,1,0:T(1,128)S(1)}, u32[]{:S(2)}, u32[]{:S(2)}) %all-to-all-start.2) | async-done | bytes 196640 | tf_op jit(solution)/shard_map/all_to_all | solution.py:31
  93.3 1.1 reduce.4
  94.4 0.1 reshape.203
  94.5 0.1 fusion.20
  94.6 0.1 reshape.199
  94.8 0.1 reshape.198
  94.9 0.0 copy-done.1
  94.9 0.3 fusion.4
  95.3 0.3 multiply_reduce_fusion.2
  95.6 0.3 fusion.8
  95.9 0.3 fusion.21
  96.2 0.1 reshape.190
  96.3 0.1 reshape.191
  96.4 0.1 pad_maximum_fusion.3
  96.5 10.5 %all_to_all.45 = f32[16,1,224]{2,1,0:T(1,128)S(1)} all-to-all(f32[16,1,224]{2,1,0:T(1,128)S(1)} %broadcast_in_dim.4), channel_id=1, replica_groups=mesh['epoch'=16,'blend'=16] {'epoch'}, dimensions={0} | all-to-all | bytes 28672 | tf_op jit(solution)/shard_map/all_to_all | solution.py:37
  107.1 0.1 slice.32
  107.2 0.1 reshape.192
  107.3 0.1 reshape.193
  107.4 0.1 multiply_add_fusion.1
  107.4 0.2 multiply_reduce_fusion.3
  107.6 0.3 fusion.9
  107.9 0.1 add_divide_fusion.2
  108.0 0.4 multiply_reduce_fusion.1
  108.4 0.3 fusion.13
  108.7 0.3 fusion.22
  109.0 0.1 reshape.194
  109.2 0.1 reshape.195
  109.2 0.1 pad_maximum_fusion.4
  109.3 0.6 broadcast_in_dim.5
  109.9 4.7 %all-to-all-start.4 = ((f32[16,1,224]{2,1,0:T(1,128)}), f32[16,1,224]{2,1,0:T(1,128)S(1)}, u32[]{:S(2)}, u32[]{:S(2)}) async-start(f32[16,1,224]{2,1,0:T(1,128)} %broadcast_in_dim.5), calls=%async_computation.4 | async-start | bytes 32768 | tf_op jit(solution)/shard_map/all_to_all | solution.py:37
  114.7 0.7 copy.112
  115.4 5.6 %all-to-all-done.4 = f32[16,1,224]{2,1,0:T(1,128)S(1)} async-done(((f32[16,1,224]{2,1,0:T(1,128)}), f32[16,1,224]{2,1,0:T(1,128)S(1)}, u32[]{:S(2)}, u32[]{:S(2)}) %all-to-all-start.4) | async-done | bytes 14368 | tf_op jit(solution)/shard_map/all_to_all | solution.py:37
  121.0 0.1 slice.34
  121.1 0.1 reshape.196
  121.2 0.1 reshape.197
  121.3 0.1 multiply_add_fusion
  121.3 0.1 add_maximum_fusion
  121.4 0.7 copy.113
  (16 shorter events, 0.3 us)
Async XLA Ops:
  56.7 11.4 %copy-start.4 = (s32[4]{0:T(128)S(1)}, s32[4]{0:T(128)}, u32[]{:S(2)}) copy-start(s32[4]{0:T(128)} %param.11) | copy-start | bytes 52
  56.7 11.4 %copy-start.3 = (f32[4,8,6]{1,0,2:T(4,128)S(1)}, f32[4,8,6]{1,0,2:T(4,128)}, u32[]{:S(2)}) copy-start(f32[4,8,6]{1,0,2:T(4,128)} %param.12) | copy-start | bytes 2308
  59.4 18.5 %all-to-all-start.1 = ((f32[16,1,3072]{2,1,0:T(1,128)}), f32[16,1,3072]{2,1,0:T(1,128)S(1)}, u32[]{:S(2)}, u32[]{:S(2)}) async-start(f32[16,1,3072]{2,1,0:T(1,128)} %reshape.200), calls=%async_computation.1 | async-start | bytes 393216 | tf_op jit(solution)/shard_map/all_to_all | solution.py:31
  79.5 15.4 %copy-start.1 = (s32[4,8,1024]{2,1,0:T(8,128)S(1)}, s32[4,8,1024]{2,1,0:T(8,128)}, u32[]{:S(2)}) copy-start(s32[4,8,1024]{2,1,0:T(8,128)} %param.10) | copy-start | bytes 393220
  79.5 15.4 %copy-start.2 = (f32[4,8,1024]{2,1,0:T(8,128)S(1)}, f32[4,8,1024]{2,1,0:T(8,128)}, u32[]{:S(2)}) copy-start(f32[4,8,1024]{2,1,0:T(8,128)} %param.13) | copy-start | bytes 393220
  80.6 12.7 %all-to-all-start.2 = ((f32[16,1,3072]{2,1,0:T(1,128)}), f32[16,1,3072]{2,1,0:T(1,128)S(1)}, u32[]{:S(2)}, u32[]{:S(2)}) async-start(f32[16,1,3072]{2,1,0:T(1,128)} %reshape.202), calls=%async_computation.2 | async-start | bytes 393216 | tf_op jit(solution)/shard_map/all_to_all | solution.py:31
  108.4 13.8 %copy-start = (f32[4,8,1024]{2,1,0:T(8,128)}, f32[4,8,1024]{2,1,0:T(8,128)S(1)}, u32[]{:S(2)}) copy-start(f32[4,8,1024]{2,1,0:T(8,128)S(1)} %get-tuple-element.34) | copy-start | bytes 393220
  109.9 11.0 %all-to-all-start.4 = ((f32[16,1,224]{2,1,0:T(1,128)}), f32[16,1,224]{2,1,0:T(1,128)S(1)}, u32[]{:S(2)}, u32[]{:S(2)}) async-start(f32[16,1,224]{2,1,0:T(1,128)} %broadcast_in_dim.5), calls=%async_computation.4 | async-start | bytes 32768 | tf_op jit(solution)/shard_map/all_to_all | solution.py:37
where the time goes:
time: 123 us; the launch traced here: 122 us
  blocking collectives  56.1 us (46%)
  waiting for transfers between devices  23.1 us (19%)
  starting transfers between devices  18.1 us (15%)
  local copies, waits for them, and re-layouts  11.3 us (9%)
  other arithmetic  10.1 us (8%)
  matrix products  2.64 us (2%)
    all_to_all x1, blocking collectives, sent_and_summed(): lax.all_to_all(pieces, axis, split_axis=0, concat_axis=0, tiled=True)  45.5 us
    all_to_all x2, waiting for transfers between devices, side_by_side_2(): lax.all_to_all(both, axis, split_axis=split_dim, concat_axis=concat_dim,...  17.5 us
    all_to_all x2, starting transfers between devices, side_by_side_2(): lax.all_to_all(both, axis, split_axis=split_dim, concat_axis=concat_dim,...  13.3 us
    all_to_all x1, blocking collectives, from_everyone(): return lax.all_to_all(copies, axis, split_axis=0, concat_axis=0, tiled=True)  10.5 us
    all_to_all x1, waiting for transfers between devices, from_everyone(): return lax.all_to_all(copies, axis, split_axis=0, concat_axis=0, tiled=True)  5.59 us
    reduce_sum x1, other arithmetic, on_device(): numerator = jnp.sum(weights * visit_flux.astype(jnp.float32), axis=0)  5.1 us
    all_to_all x1, starting transfers between devices, from_everyone(): return lax.all_to_all(copies, axis, split_axis=0, concat_axis=0, tiled=True)  4.74 us
    unnamed x18, local copies, waits for them, and re-layouts  4.22 us
  transfers between devices with their start and end apart: 3, of which 3 were waited for; matrix products, arithmetic and copies ran while one was open for 1% of the time, Pallas kernels for 0%

commit v1 on v0

v1 whole, which is shorter than its diff:
```python
import jax
import jax.numpy as jnp
from jax import lax
from jax.experimental import pallas as pl
from jax.experimental.pallas import tpu as pltpu
from jax.sharding import PartitionSpec as P

ITERS = 2
F32 = jnp.float32
FIRST = (0, 2)
SECOND = (1, 3, 4, 5, 6, 7)
VMEM = pl.BlockSpec(memory_space=pltpu.VMEM)
ANY = pl.BlockSpec(memory_space=pl.ANY)


def visit_kernel(pairs, flux_ref, prec_ref, live_ref, *rest):
    outs, (flux_buf, prec_buf, sems) = rest[: 2 * len(pairs)], rest[2 * len(pairs) :]
    e = lax.axis_index("epoch")
    odd = lax.rem(e, 2) == 1
    visits, bands = flux_buf.shape[1], flux_buf.shape[2]
    width = flux_buf.shape[4]
    copies = []
    starts = []
    for n, j in enumerate(pairs):
        start = pl.multiple_of(lax.bitwise_xor(lax.div(e, 2), j) * 8, 8)
        starts.append(start)
        a = pltpu.make_async_copy(flux_ref.at[:, :, pl.ds(start, 8), :], flux_buf.at[n], sems.at[0, n])
        b = pltpu.make_async_copy(prec_ref.at[:, :, pl.ds(start, 8), :], prec_buf.at[n], sems.at[1, n])
        a.start()
        b.start()
        copies.append((a, b))
    low_rows = lax.broadcasted_iota(jnp.int32, (8, 128), 0) < 4
    for n in range(len(pairs)):
        for copy in copies[n]:
            copy.wait()
        lives = [live_ref[v, pl.ds(starts[n], 8), :] for v in range(visits)]
        even_out, odd_out = outs[2 * n], outs[2 * n + 1]

        def lane_tile(l, _, n=n, lives=lives, even_out=even_out, odd_out=odd_out):
            lanes = pl.ds(pl.multiple_of(l * 128, 128), 128)
            for cc in range(bands // 2):
                sums = []
                for c in (2 * cc, 2 * cc + 1):
                    num = jnp.zeros((8, 128), F32)
                    wsum = jnp.zeros((8, 128), F32)
                    for v in range(visits):
                        w = prec_buf[n, v, c, :, lanes].astype(F32) * lives[v]
                        num = num + w * flux_buf[n, v, c, :, lanes].astype(F32)
                        wsum = wsum + w
                    sums.append((num, wsum))
                for q in range(2):
                    first, second = sums[0][q], sums[1][q]
                    low = jnp.where(low_rows, first, pltpu.roll(second, 4, 0))
                    high = jnp.where(low_rows, pltpu.roll(first, 4, 0), second)
                    even_out[q * (bands // 2) + cc, :, lanes] = jnp.where(odd, high, low)
                    odd_out[q * (bands // 2) + cc, :, lanes] = jnp.where(odd, low, high)
            return 0

        lax.fori_loop(0, width // 128, lane_tile, 0)


def visit_sums(pairs, flux, prec, live):
    visits, bands, _, width = flux.shape
    piece = jax.ShapeDtypeStruct((bands, 8, width), F32)
    buf = pltpu.VMEM((len(pairs), visits, bands, 8, width), flux.dtype)
    work = visits * bands * 8 * len(pairs) * width
    return pl.pallas_call(
        lambda *refs: visit_kernel(pairs, *refs),
        out_shape=[piece] * (2 * len(pairs)),
        in_specs=[ANY, ANY, VMEM],
        out_specs=[VMEM] * (2 * len(pairs)),
        scratch_shapes=[buf, buf, pltpu.SemaphoreType.DMA((2, len(pairs)))],
        compiler_params=pltpu.CompilerParams(vmem_limit_bytes=20 * 2**20),
        cost_estimate=pl.CostEstimate(flops=8 * work, bytes_accessed=4 * work, transcendentals=0),
        name="visit_sums_%d" % len(pairs),
    )(flux, prec, live)


def spread(tile, n):
    return jnp.broadcast_to(tile[:, n : n + 1], tile.shape)


def step_body(s, many, coadd_ref, cover_ref, morph, mask_ref, morph_out, resid_ref, payload_ref):
    halves, width = resid_ref.shape[0], resid_ref.shape[2]
    slots = mask_ref.shape[0]
    sb = [[spread(s, cc * slots + k) for cc in range(halves)] for k in range(slots)]
    steps = []
    for k in range(slots):
        sq = sb[k][0] * sb[k][0]
        for cc in range(1, halves):
            sq = sq + sb[k][cc] * sb[k][cc]
        sq = sq + pltpu.roll(sq, 4, 0)
        steps.append(1.0 / (1.0 + many * sq))

    def residual(ms, cc, lanes):
        model = sb[0][cc] * ms[0]
        for k in range(1, slots):
            model = model + sb[k][cc] * ms[k]
        return cover_ref[cc, :, lanes] * (coadd_ref[cc, :, lanes] - model)

    def lane_tile(l, _):
        lanes = pl.ds(pl.multiple_of(l * 128, 128), 128)
        ms = [morph[k, :, lanes] for k in range(slots)]
        rs = [residual(ms, cc, lanes) for cc in range(halves)]
        new = []
        for k in range(slots):
            grad = sb[k][0] * rs[0]
            for cc in range(1, halves):
                grad = grad + sb[k][cc] * rs[cc]
            grad = grad + pltpu.roll(grad, 4, 0)
            m = jnp.maximum(0.0, ms[k] + grad * steps[k]) * mask_ref[k, :, lanes]
            morph_out[k, :, lanes] = m
            new.append(m)
        for cc in range(halves):
            resid_ref[cc, :, lanes] = residual(new, cc, lanes)
        return 0

    lax.fori_loop(0, width // 128, lane_tile, 0)
    lane = lax.broadcasted_iota(jnp.int32, (8, 128), 1)
    total = jnp.zeros((8, 128), F32)
    rs = [resid_ref[cc] for cc in range(halves)]
    for k in range(slots):
        m = morph_out[k]
        for cc in range(halves):
            got = jnp.sum(m * rs[cc], axis=1, keepdims=True)
            total = jnp.where(lane == cc * slots + k, got, total)
        got = jnp.sum(m * m, axis=1, keepdims=True)
        total = jnp.where(lane == halves * slots + k, got, total)
    for n in range(payload_ref.shape[0]):
        payload_ref[n] = total


def spectra_step(s, many, arrived_ref, halves, slots):
    total = arrived_ref[0]
    for n in range(1, arrived_ref.shape[0]):
        total = total + arrived_ref[n]
    lane = lax.broadcasted_iota(jnp.int32, (8, 128), 1)
    norm = total
    for cc in range(halves):
        moved = pltpu.roll(total, 128 - (halves - cc) * slots, 1)
        norm = jnp.where((lane >= cc * slots) & (lane < (cc + 1) * slots), moved, norm)
    new = jnp.maximum(0.0, s + total / (1.0 + many * norm))
    return jnp.where(lane < halves * slots, new, 0.0)


def first_kernel(sums_ref, mask_ref, morph_ref, s_ref, many_ref, coadd_ref, cover_ref, morph_out, payload_ref, resid_ref):
    halves = coadd_ref.shape[0]
    width = coadd_ref.shape[2]

    def lane_tile(l, _):
        lanes = pl.ds(pl.multiple_of(l * 128, 128), 128)
        for cc in range(halves):
            wsum = sums_ref[halves + cc, :, lanes]
            below = 1.0 / (1.0 + wsum)
            coadd_ref[cc, :, lanes] = sums_ref[cc, :, lanes] * below
            cover_ref[cc, :, lanes] = wsum * below
        return 0

    lax.fori_loop(0, width // 128, lane_tile, 0)
    step_body(s_ref[...], many_ref[...], coadd_ref, cover_ref, morph_ref, mask_ref, morph_out, resid_ref, payload_ref)


def next_kernel(arrived_ref, s_ref, many_ref, coadd_ref, cover_ref, morph_ref, mask_ref, s_out, morph_out, payload_ref, resid_ref):
    halves, slots = coadd_ref.shape[0], mask_ref.shape[0]
    s = spectra_step(s_ref[...], many_ref[...], arrived_ref, halves, slots)
    s_out[...] = s
    step_body(s, many_ref[...], coadd_ref, cover_ref, morph_ref, mask_ref, morph_out, resid_ref, payload_ref)


def last_kernel(arrived_ref, s_ref, many_ref, out_ref):
    bands, owned, slots = out_ref.shape
    s = spectra_step(s_ref[...], many_ref[...], arrived_ref, bands // 2, slots)
    for c in range(bands):
        out_ref[c] = s[(c % 2) * owned : (c % 2 + 1) * owned, (c // 2) * slots : (c // 2 + 1) * slots]


def call(kernel, outs, args, scratch=(), name=None):
    return pl.pallas_call(
        kernel,
        out_shape=[jax.ShapeDtypeStruct(o, F32) for o in outs],
        in_specs=[VMEM] * len(args),
        out_specs=[VMEM] * len(outs),
        scratch_shapes=[pltpu.VMEM(s, F32) for s in scratch],
        compiler_params=pltpu.CompilerParams(vmem_limit_bytes=8 * 2**20),
        cost_estimate=pl.CostEstimate(flops=4_000_000, bytes_accessed=1_000_000, transcendentals=0),
        name=name,
    )(*args)


def on_device(visit_flux, visit_precision, visit_live, footprint, source_count, spectra_init, morphology_init):
    n_epoch, n_blend = lax.axis_size("epoch"), lax.axis_size("blend")
    owned, slots, width = footprint.shape
    bands = visit_flux.shape[2]
    halves = bands // 2
    flux = jnp.transpose(visit_flux, (0, 2, 1, 3))
    prec = jnp.transpose(visit_precision, (0, 2, 1, 3))
    live = jnp.broadcast_to(visit_live.astype(F32)[:, :, None], (*visit_live.shape, 128))
    pieces = [None] * n_epoch
    for pairs in (FIRST, SECOND):
        got = visit_sums(pairs, flux, prec, live)
        for n, j in enumerate(pairs):
            pieces[2 * j], pieces[2 * j + 1] = got[2 * n], got[2 * n + 1]
    total = pieces[0]
    for m in range(1, n_epoch):
        total = total + lax.ppermute(pieces[m], "epoch", [(e, e ^ m) for e in range(n_epoch)])
    swap = [(a * n_blend + b, b * n_blend + a) for a in range(n_epoch) for b in range(n_blend)]
    sums = lax.ppermute(total, ("epoch", "blend"), swap)

    source_live = (jnp.arange(slots, dtype=jnp.int32)[None, :] < source_count[:, None]).astype(F32)
    mask = footprint.astype(F32) * source_live[:, :, None]
    twice = lambda a: jnp.concatenate([a, a], axis=1)
    mask_t = twice(jnp.transpose(mask, (1, 0, 2)))
    morph_t = twice(jnp.transpose(morphology_init * mask, (1, 0, 2)))
    many = jnp.broadcast_to(jnp.tile(source_count.astype(F32), 2)[:, None], (8, 128))
    s = jnp.transpose(spectra_init.reshape(owned, slots, halves, 2), (3, 0, 2, 1)).reshape(2 * owned, halves * slots)
    s = jnp.pad(s, ((0, 0), (0, 128 - halves * slots)))

    tile3, tile8 = (halves, 8, width), (slots, 8, width)
    payload = (n_epoch, 8, 128)
    coadd, cover, morph, sent = call(
        first_kernel, [tile3, tile3, tile8, payload], [sums, mask_t, morph_t, s, many], [tile3], "deblend_first"
    )
    swap_all = lambda a: lax.all_to_all(a, "epoch", split_axis=0, concat_axis=0, tiled=True)
    s, morph, sent = call(
        next_kernel,
        [(8, 128), tile8, payload],
        [swap_all(sent), s, many, coadd, cover, morph, mask_t],
        [tile3],
        "deblend_next",
    )
    (spectra,) = call(last_kernel, [(bands, owned, slots)], [swap_all(sent), s, many], (), "deblend_last")
    coadd = jnp.transpose(coadd.reshape(bands, owned, width), (1, 0, 2))
    return coadd, jnp.transpose(spectra, (1, 2, 0)), jnp.transpose(morph[:, :owned], (1, 0, 2))


def solution(mesh):
    in_specs = (
        P("epoch", None, None, "blend"),
        P("epoch", None, None, "blend"),
        P("epoch", None),
        P("blend", None, "epoch"),
        P("blend"),
        P("blend", None, None),
        P("blend", None, "epoch"),
    )
    out_specs = (P("blend", None, "epoch"), P("blend", None, None), P("blend", None, "epoch"))
    return jax.shard_map(
        on_device, mesh=mesh, in_specs=in_specs, out_specs=out_specs, check_vma=False
    )
```

time: 123 us -> 127 us (1.033)
  blocking collectives: 56.1 us -> 0 us
  starting transfers between devices: 18.1 us -> 66.2 us
  waiting for transfers between devices: 23.1 us -> 46.3 us
  other arithmetic: 10.1 us -> 1.19 us
  Pallas kernels: 0 us -> 6.17 us
  local copies, waits for them, and re-layouts: 11.3 us -> 5.56 us
  matrix products: 2.64 us -> 0 us
    all_to_all x2 -> x0, blocking collectives: 56.1 us -> none  [the longest x1 45.5 us: sent_and_summed(): lax.all_to_all(pieces, axis, split_axis=0, concat_axis=0, tiled=True)]
    ppermute x0 -> x16, waiting for transfers between devices: none -> 35 us  [the longest x15 31.5 us: on_device(): lax.ppermute(pieces[m], 'epoch', [(e, e ^ m) for e in range(n_epoch)])]
    ppermute x0 -> x16, starting transfers between devices: none -> 31.8 us  [the longest x15 28.9 us: on_device(): lax.ppermute(pieces[m], 'epoch', [(e, e ^ m) for e in range(n_epoch)])]
    all_to_all x3 -> x2, starting transfers between devices: 18.1 us -> 34.4 us  [on_device(): lax.all_to_all(a, 'epoch', split_axis=0, concat_axis=0, tiled=True)]
    all_to_all x3 -> x2, waiting for transfers between devices: 23.1 us -> 11.2 us  [on_device(): lax.all_to_all(a, 'epoch', split_axis=0, concat_axis=0, tiled=True)]
    pallas_call x0 -> x5, Pallas kernels: none -> 6.17 us  [the longest x3 3.32 us: call(): pl.pallas_call(kernel, out_shape=[jax.ShapeDtypeStruct(o, F32) for o in o...]
    reduce_sum x6 -> x0, other arithmetic: 5.54 us -> none  [the longest x1 5.1 us: on_device(): numerator = jnp.sum(weights * visit_flux.astype(jnp.float32), axis=0)]
    concatenate x2 -> x0, local copies, waits for them, and re-layouts: 2.88 us -> none  [the longest x1 2.37 us: side_by_side(): both = jnp.concatenate(arrays, axis=along)]
  transfers between devices with their start and end apart: 3 -> 18, of which waited for: 3 -> 8; matrix products, arithmetic and copies ran while one was open for 1% -> 1% of each run, Pallas kernels for 0% -> 1%
where the time goes in v1:
time: 127 us; the launch traced here: 126 us
  starting transfers between devices  66.2 us (52%)
  waiting for transfers between devices  46.3 us (36%)
  Pallas kernels  6.17 us (5%)
  local copies, waits for them, and re-layouts  5.56 us (4%)
    all_to_all x2, starting transfers between devices, on_device(): lax.all_to_all(a, 'epoch', split_axis=0, concat_axis=0, tiled=True)  34.4 us
    ppermute x15, waiting for transfers between devices, on_device(): lax.ppermute(pieces[m], 'epoch', [(e, e ^ m) for e in range(n_epoch)])  31.5 us
    ppermute x15, starting transfers between devices, on_device(): lax.ppermute(pieces[m], 'epoch', [(e, e ^ m) for e in range(n_epoch)])  28.9 us
    all_to_all x2, waiting for transfers between devices, on_device(): lax.all_to_all(a, 'epoch', split_axis=0, concat_axis=0, tiled=True)  11.2 us
    unnamed x13, local copies, waits for them, and re-layouts  4.54 us
    ppermute x1, waiting for transfers between devices, on_device(): sums = lax.ppermute(total, ('epoch', 'blend'), swap)  3.58 us
    pallas_call x3, Pallas kernels, call(): pl.pallas_call(kernel, out_shape=[jax.ShapeDtypeStruct(o, F32) for o in o...  3.32 us
    ppermute x1, starting transfers between devices, on_device(): sums = lax.ppermute(total, ('epoch', 'blend'), swap)  2.89 us
  transfers between devices with their start and end apart: 18, of which 8 were waited for; matrix products, arithmetic and copies ran while one was open for 1% of the time, Pallas kernels for 1%

profile of v1, /device:TPU:2, one launch (start us, length us, event | category | flops | bytes accessed | tf_op | source)
XLA Modules:
  0.0 126.2 jit_solution(4809754995616337163)
XLA Ops:
  0.6 0.7 convert_element_type.18
  1.3 0.1 broadcast_in_dim.6.refs_2_
  1.4 0.0 copy-start
  1.4 1.9 %copy-done = bf16[4,64,6,1024]{3,1,2,0:T(8,128)(2,1)S(1)} copy-done((bf16[4,64,6,1024]{3,1,2,0:T(8,128)(2,1)S(1)}, bf16[4,64,6,1024]{3,1,2,0:T(8,128)(2,1)}, u32[]{:S(2)}) %copy-start) | copy-done | bytes 3145752
  3.3 0.0 copy-start.1
  3.3 1.9 %copy-done.1 = bf16[4,64,6,1024]{3,1,2,0:T(8,128)(2,1)S(1)} copy-done((bf16[4,64,6,1024]{3,1,2,0:T(8,128)(2,1)S(1)}, bf16[4,64,6,1024]{3,1,2,0:T(8,128)(2,1)}, u32[]{:S(2)}) %copy-start.1) | copy-done | bytes 3145752
  5.2 2.1 %visit_sums_6.1 = (f32[6,8,1024]{2,1,0:T(8,128)S(1)}, f32[6,8,1024]{2,1,0:T(8,128)S(1)}, f32[6,8,1024]{2,1,0:T(8,128)S(1)}, f32[6,8,1024]{2,1,0:T(8,128)S(1)}, f...) custom-call(bf16[4,6,64,1024]{3,2,1,0:T(8,128)(2,1)S(1)} %bitcast.14, ...), custom_call_target="tpu_custom_call" | custom-call | flops 9437184 | bytes 4718592 | tf_op jit(solution)/shard_map/visit_sums_6/pallas_call | solution.py:67
  7.3 2.2 %collective-permute-start.1 = (f32[6,8,1024]{2,1,0:T(8,128)S(1)}, f32[6,8,1024]{2,1,0:T(8,128)S(1)}, u32[]{:S(2)}, u32[]{:S(2)}) collective-permute-start(f32[6,8,1024]{2,1,0:T(8,128)S(1)} %get-tuple-element.28), channel_id=1, source_target_pairs={{0,32},{16,48},{32,0},{48,16},{64,96},{80,112},{96,64},{112,80},{1... | collective-permute-start | bytes 589832 | tf_op jit(solution)/shard_map/ppermute | solution.py:205
  9.6 2.5 %collective-permute-start.10 = (f32[6,8,1024]{2,1,0:T(8,128)S(1)}, f32[6,8,1024]{2,1,0:T(8,128)S(1)}, u32[]{:S(2)}, u32[]{:S(2)}) collective-permute-start(f32[6,8,1024]{2,1,0:T(8,128)S(1)} %get-tuple-element.37), channel_id=1, source_target_pairs={{0,176},{16,160},{32,144},{48,128},{64,240},{80,224},{96,208},{112... | collective-permute-start | bytes 589832 | tf_op jit(solution)/shard_map/ppermute | solution.py:205
  12.1 1.1 collective-permute-start.11
  13.1 4.3 %collective-permute-start.12 = (f32[6,8,1024]{2,1,0:T(8,128)S(1)}, f32[6,8,1024]{2,1,0:T(8,128)S(1)}, u32[]{:S(2)}, u32[]{:S(2)}) collective-permute-start(f32[6,8,1024]{2,1,0:T(8,128)S(1)} %get-tuple-element.39), channel_id=1, source_target_pairs={{0,208},{16,192},{32,240},{48,224},{64,144},{80,128},{96,176},{112... | collective-permute-start | bytes 589832 | tf_op jit(solution)/shard_map/ppermute | solution.py:205
  17.4 1.4 %collective-permute-start.13 = (f32[6,8,1024]{2,1,0:T(8,128)S(1)}, f32[6,8,1024]{2,1,0:T(8,128)S(1)}, u32[]{:S(2)}, u32[]{:S(2)}) collective-permute-start(f32[6,8,1024]{2,1,0:T(8,128)S(1)} %get-tuple-element.40), channel_id=1, source_target_pairs={{0,224},{16,240},{32,192},{48,208},{64,160},{80,176},{96,128},{112... | collective-permute-start | bytes 589832 | tf_op jit(solution)/shard_map/ppermute | solution.py:205
  18.8 0.0 collective-permute-done.1
  18.8 1.5 %collective-permute-start.14 = (f32[6,8,1024]{2,1,0:T(8,128)S(1)}, f32[6,8,1024]{2,1,0:T(8,128)S(1)}, u32[]{:S(2)}, u32[]{:S(2)}) collective-permute-start(f32[6,8,1024]{2,1,0:T(8,128)S(1)} %get-tuple-element.41), channel_id=1, source_target_pairs={{0,240},{16,224},{32,208},{48,192},{64,176},{80,160},{96,144},{112... | collective-permute-start | bytes 589832 | tf_op jit(solution)/shard_map/ppermute | solution.py:205
  20.4 6.3 %collective-permute-done.10 = f32[6,8,1024]{2,1,0:T(8,128)S(1)} collective-permute-done((f32[6,8,1024]{2,1,0:T(8,128)S(1)}, f32[6,8,1024]{2,1,0:T(8,128)S(1)}, u32[]{:S(2)}, u32[]{:S(2)}) %collective-permute-start.10) | collective-permute-done | bytes 196640 | tf_op jit(solution)/shard_map/ppermute | solution.py:205
  26.7 0.0 collective-permute-start.2
  26.7 9.4 %collective-permute-done.11 = f32[6,8,1024]{2,1,0:T(8,128)S(1)} collective-permute-done((f32[6,8,1024]{2,1,0:T(8,128)S(1)}, f32[6,8,1024]{2,1,0:T(8,128)S(1)}, u32[]{:S(2)}, u32[]{:S(2)}) %collective-permute-start.11) | collective-permute-done | bytes 196640 | tf_op jit(solution)/shard_map/ppermute | solution.py:205
  36.1 2.6 %collective-permute-start.5 = (f32[6,8,1024]{2,1,0:T(8,128)S(1)}, f32[6,8,1024]{2,1,0:T(8,128)S(1)}, u32[]{:S(2)}, u32[]{:S(2)}) collective-permute-start(f32[6,8,1024]{2,1,0:T(8,128)S(1)} %get-tuple-element.32), channel_id=1, source_target_pairs={{0,96},{16,112},{32,64},{48,80},{64,32},{80,48},{96,0},{112,16},{1... | collective-permute-start | bytes 589832 | tf_op jit(solution)/shard_map/ppermute | solution.py:205
  38.7 0.0 collective-permute-done.12
  38.7 2.4 %collective-permute-start.6 = (f32[6,8,1024]{2,1,0:T(8,128)S(1)}, f32[6,8,1024]{2,1,0:T(8,128)S(1)}, u32[]{:S(2)}, u32[]{:S(2)}) collective-permute-start(f32[6,8,1024]{2,1,0:T(8,128)S(1)} %get-tuple-element.33), channel_id=1, source_target_pairs={{0,112},{16,96},{32,80},{48,64},{64,48},{80,32},{96,16},{112,0},{1... | collective-permute-start | bytes 589832 | tf_op jit(solution)/shard_map/ppermute | solution.py:205
  41.2 0.0 collective-permute-done.13
  41.2 0.0 copy-start.5
  41.2 0.7 collective-permute-start.7
  41.9 0.7 visit_sums_2.1
  42.6 0.0 copy-start.2
  42.6 0.0 copy-start.3
  42.6 0.0 copy-start.4
  42.7 0.0 collective-permute-done.14
  42.7 2.9 %collective-permute-start.8 = (f32[6,8,1024]{2,1,0:T(8,128)S(1)}, f32[6,8,1024]{2,1,0:T(8,128)S(1)}, u32[]{:S(2)}, u32[]{:S(2)}) collective-permute-start(f32[6,8,1024]{2,1,0:T(8,128)S(1)} %get-tuple-element.35), channel_id=1, source_target_pairs={{0,144},{16,128},{32,176},{48,160},{64,208},{80,192},{96,240},{112... | collective-permute-start | bytes 589832 | tf_op jit(solution)/shard_map/ppermute | solution.py:205
  45.5 0.0 collective-permute-done.2
  45.5 1.9 %collective-permute-start.9 = (f32[6,8,1024]{2,1,0:T(8,128)S(1)}, f32[6,8,1024]{2,1,0:T(8,128)S(1)}, u32[]{:S(2)}, u32[]{:S(2)}) collective-permute-start(f32[6,8,1024]{2,1,0:T(8,128)S(1)} %get-tuple-element.36), channel_id=1, source_target_pairs={{0,160},{16,176},{32,128},{48,144},{64,224},{80,240},{96,192},{112... | collective-permute-start | bytes 589832 | tf_op jit(solution)/shard_map/ppermute | solution.py:205
  47.4 0.0 collective-permute-done.5
  47.4 1.7 %collective-permute-start = (f32[6,8,1024]{2,1,0:T(8,128)S(1)}, f32[6,8,1024]{2,1,0:T(8,128)S(1)}, u32[]{:S(2)}, u32[]{:S(2)}) collective-permute-start(f32[6,8,1024]{2,1,0:T(8,128)S(1)} %get-tuple-element.27), channel_id=1, source_target_pairs={{0,16},{16,0},{32,48},{48,32},{64,80},{80,64},{96,112},{112,96},{1... | collective-permute-start | bytes 589832 | tf_op jit(solution)/shard_map/ppermute | solution.py:205
  49.1 0.7 collective-permute-done.6
  49.8 1.5 %collective-permute-start.3 = (f32[6,8,1024]{2,1,0:T(8,128)S(1)}, f32[6,8,1024]{2,1,0:T(8,128)S(1)}, u32[]{:S(2)}, u32[]{:S(2)}) collective-permute-start(f32[6,8,1024]{2,1,0:T(8,128)S(1)} %get-tuple-element.30), channel_id=1, source_target_pairs={{0,64},{16,80},{32,96},{48,112},{64,0},{80,16},{96,32},{112,48},{1... | collective-permute-start | bytes 589832 | tf_op jit(solution)/shard_map/ppermute | solution.py:205
  51.3 9.2 %collective-permute-done.7 = f32[6,8,1024]{2,1,0:T(8,128)S(1)} collective-permute-done((f32[6,8,1024]{2,1,0:T(8,128)S(1)}, f32[6,8,1024]{2,1,0:T(8,128)S(1)}, u32[]{:S(2)}, u32[]{:S(2)}) %collective-permute-start.7) | collective-permute-done | bytes 196640 | tf_op jit(solution)/shard_map/ppermute | solution.py:205
  60.5 2.2 %collective-permute-start.4 = (f32[6,8,1024]{2,1,0:T(8,128)S(1)}, f32[6,8,1024]{2,1,0:T(8,128)S(1)}, u32[]{:S(2)}, u32[]{:S(2)}) collective-permute-start(f32[6,8,1024]{2,1,0:T(8,128)S(1)} %get-tuple-element.31), channel_id=1, source_target_pairs={{0,80},{16,64},{32,112},{48,96},{64,16},{80,0},{96,48},{112,32},{1... | collective-permute-start | bytes 589832 | tf_op jit(solution)/shard_map/ppermute | solution.py:205
  62.7 0.0 copy-done.5
  62.7 0.0 collective-permute-done.8
  62.7 0.0 collective-permute-done.9
  62.7 0.0 collective-permute-done
  62.7 5.8 %collective-permute-done.3 = f32[6,8,1024]{2,1,0:T(8,128)S(1)} collective-permute-done((f32[6,8,1024]{2,1,0:T(8,128)S(1)}, f32[6,8,1024]{2,1,0:T(8,128)S(1)}, u32[]{:S(2)}, u32[]{:S(2)}) %collective-permute-start.3) | collective-permute-done | bytes 196640 | tf_op jit(solution)/shard_map/ppermute | solution.py:205
  68.5 0.0 collective-permute-done.4
  68.5 0.2 add_add_fusion
  68.8 2.9 %collective-permute-start.15 = (f32[6,8,1024]{2,1,0:T(8,128)S(1)}, f32[6,8,1024]{2,1,0:T(8,128)S(1)}, u32[]{:S(2)}, u32[]{:S(2)}) collective-permute-start(f32[6,8,1024]{2,1,0:T(8,128)S(1)} %add_add_fusion), channel_id=1, source_target_pairs={{0,0},{1,16},{2,32},{3,48},{4,64},{5,80},{6,96},{7,112},{8,128},{9... | collective-permute-start | bytes 589832 | tf_op jit(solution)/shard_map/ppermute | solution.py:207
  71.7 0.0 copy-done.2
  71.7 0.0 copy-done.3
  71.7 0.2 fusion
  71.9 0.1 broadcast_in_dim.7
  72.0 0.0 copy-done.4
  72.0 0.1 reshape.41
  72.1 0.1 pad_maximum_fusion
  72.2 3.6 %collective-permute-done.15.sums_ref = f32[6,8,1024]{2,1,0:T(8,128)S(1)} collective-permute-done((f32[6,8,1024]{2,1,0:T(8,128)S(1)}, f32[6,8,1024]{2,1,0:T(8,128)S(1)}, u32[]{:S(2)}, u32[]{:S(2)}) %collective-permute-start.15) | collective-permute-done | bytes 196640 | tf_op jit(solution)/shard_map/ppermute | solution.py:207
  75.8 0.1 broadcast_in_dim.8.many_ref
  75.8 1.3 %deblend_first.1 = (f32[3,8,1024]{2,1,0:T(8,128)S(1)}, f32[3,8,1024]{2,1,0:T(8,128)S(1)}, f32[8,8,1024]{2,1,0:T(8,128)S(1)}, f32[16,8,128]{2,1,0:T(8,128)}) custom-call(f32[6,8,1024]{2,1,0:T(8,128)S(1)} %collective-permute-done.15.sums_ref, f32[8,8,1024]{2,1,0:T(8,128)S(1)} %get-tuple-element.57.mask_ref, f32[8,8,1024]{2,1,0:T(8,128)S(1)} %get-tuple-element.58.morph_ref, ...), custom_call_target="tpu_custom_call" | custom-call | flops 4000000 | bytes 1000000 | tf_op jit(solution)/shard_map/deblend_first/pallas_call | solution.py:178
  77.1 29.7 %all-to-all-start = ((f32[16,8,128]{2,1,0:T(8,128)}), f32[16,8,128]{2,1,0:T(8,128)S(1)}, u32[]{:S(2)}, u32[]{:S(2)}) async-start(f32[16,8,128]{2,1,0:T(8,128)} %get-tuple-element.43), calls=%async_computation | async-start | bytes 131072 | tf_op jit(solution)/shard_map/all_to_all | solution.py:223
  106.8 0.7 reshape.42
  107.4 5.6 %all-to-all-done.arrived_ref = f32[16,8,128]{2,1,0:T(8,128)S(1)} async-done(((f32[16,8,128]{2,1,0:T(8,128)}), f32[16,8,128]{2,1,0:T(8,128)S(1)}, u32[]{:S(2)}, u32[]{:S(2)}) %all-to-all-start) | async-done | bytes 65568 | tf_op jit(solution)/shard_map/all_to_all | solution.py:223
  113.1 1.3 %deblend_next.1 = (f32[8,128]{1,0:T(8,128)S(1)}, f32[8,8,1024]{2,1,0:T(8,128)S(1)}, f32[16,8,128]{2,1,0:T(8,128)}) custom-call(f32[16,8,128]{2,1,0:T(8,128)S(1)} %all-to-all-done.arrived_ref, f32[8,128]{1,0:T(8,128)S(1)} %pad.4.s_ref, f32[8,128]{1,0:T(8,128)S(1)} %broadcast_in_dim.8.many_ref, f32[3,8,1024]{2,1,0:T(8,128)S(1)} %get-tuple-element.42.coadd_ref, ...), custom_call_target="tpu_custom_call" | custom-call | flops 4000000 | bytes 1000000 | tf_op jit(solution)/shard_map/deblend_next/pallas_call | solution.py:178
  114.3 4.7 %all-to-all-start.1 = ((f32[16,8,128]{2,1,0:T(8,128)}), f32[16,8,128]{2,1,0:T(8,128)S(1)}, u32[]{:S(2)}, u32[]{:S(2)}) async-start(f32[16,8,128]{2,1,0:T(8,128)} %get-tuple-element.46), calls=%async_computation.1 | async-start | bytes 131072 | tf_op jit(solution)/shard_map/all_to_all | solution.py:223
  119.1 0.7 copy.17
  119.8 5.6 %all-to-all-done.1.arrived_ref = f32[16,8,128]{2,1,0:T(8,128)S(1)} async-done(((f32[16,8,128]{2,1,0:T(8,128)}), f32[16,8,128]{2,1,0:T(8,128)S(1)}, u32[]{:S(2)}, u32[]{:S(2)}) %all-to-all-start.1) | async-done | bytes 65568 | tf_op jit(solution)/shard_map/all_to_all | solution.py:223
  125.5 0.8 deblend_last.1
  (6 shorter events, 0.0 us)
Async XLA Ops:
  1.4 1.9 %copy-start = (bf16[4,64,6,1024]{3,1,2,0:T(8,128)(2,1)S(1)}, bf16[4,64,6,1024]{3,1,2,0:T(8,128)(2,1)}, u32[]{:S(2)}) copy-start(bf16[4,64,6,1024]{3,1,2,0:T(8,128)(2,1)} %param.7) | copy-start | bytes 9437188
  3.3 1.9 %copy-start.1 = (bf16[4,64,6,1024]{3,1,2,0:T(8,128)(2,1)S(1)}, bf16[4,64,6,1024]{3,1,2,0:T(8,128)(2,1)}, u32[]{:S(2)}) copy-start(bf16[4,64,6,1024]{3,1,2,0:T(8,128)(2,1)} %param.8) | copy-start | bytes 9437188
  7.3 11.5 %collective-permute-start.1 = (f32[6,8,1024]{2,1,0:T(8,128)S(1)}, f32[6,8,1024]{2,1,0:T(8,128)S(1)}, u32[]{:S(2)}, u32[]{:S(2)}) collective-permute-start(f32[6,8,1024]{2,1,0:T(8,128)S(1)} %get-tuple-element.28), channel_id=1, source_target_pairs={{0,32},{16,48},{32,0},{48,16},{64,96},{80,112},{96,64},{112,80},{1... | collective-permute-start | bytes 589832 | tf_op jit(solution)/shard_map/ppermute | solution.py:205
  9.6 17.2 %collective-permute-start.10 = (f32[6,8,1024]{2,1,0:T(8,128)S(1)}, f32[6,8,1024]{2,1,0:T(8,128)S(1)}, u32[]{:S(2)}, u32[]{:S(2)}) collective-permute-start(f32[6,8,1024]{2,1,0:T(8,128)S(1)} %get-tuple-element.37), channel_id=1, source_target_pairs={{0,176},{16,160},{32,144},{48,128},{64,240},{80,224},{96,208},{112... | collective-permute-start | bytes 589832 | tf_op jit(solution)/shard_map/ppermute | solution.py:205
  12.1 24.0 %collective-permute-start.11 = (f32[6,8,1024]{2,1,0:T(8,128)S(1)}, f32[6,8,1024]{2,1,0:T(8,128)S(1)}, u32[]{:S(2)}, u32[]{:S(2)}) collective-permute-start(f32[6,8,1024]{2,1,0:T(8,128)S(1)} %get-tuple-element.38), channel_id=1, source_target_pairs={{0,192},{16,208},{32,224},{48,240},{64,128},{80,144},{96,160},{112... | collective-permute-start | bytes 589832 | tf_op jit(solution)/shard_map/ppermute | solution.py:205
  13.1 25.6 %collective-permute-start.12 = (f32[6,8,1024]{2,1,0:T(8,128)S(1)}, f32[6,8,1024]{2,1,0:T(8,128)S(1)}, u32[]{:S(2)}, u32[]{:S(2)}) collective-permute-start(f32[6,8,1024]{2,1,0:T(8,128)S(1)} %get-tuple-element.39), channel_id=1, source_target_pairs={{0,208},{16,192},{32,240},{48,224},{64,144},{80,128},{96,176},{112... | collective-permute-start | bytes 589832 | tf_op jit(solution)/shard_map/ppermute | solution.py:205
  17.4 23.7 %collective-permute-start.13 = (f32[6,8,1024]{2,1,0:T(8,128)S(1)}, f32[6,8,1024]{2,1,0:T(8,128)S(1)}, u32[]{:S(2)}, u32[]{:S(2)}) collective-permute-start(f32[6,8,1024]{2,1,0:T(8,128)S(1)} %get-tuple-element.40), channel_id=1, source_target_pairs={{0,224},{16,240},{32,192},{48,208},{64,160},{80,176},{96,128},{112... | collective-permute-start | bytes 589832 | tf_op jit(solution)/shard_map/ppermute | solution.py:205
  18.8 23.8 %collective-permute-start.14 = (f32[6,8,1024]{2,1,0:T(8,128)S(1)}, f32[6,8,1024]{2,1,0:T(8,128)S(1)}, u32[]{:S(2)}, u32[]{:S(2)}) collective-permute-start(f32[6,8,1024]{2,1,0:T(8,128)S(1)} %get-tuple-element.41), channel_id=1, source_target_pairs={{0,240},{16,224},{32,208},{48,192},{64,176},{80,160},{96,144},{112... | collective-permute-start | bytes 589832 | tf_op jit(solution)/shard_map/ppermute | solution.py:205
  26.7 18.8 %collective-permute-start.2 = (f32[6,8,1024]{2,1,0:T(8,128)S(1)}, f32[6,8,1024]{2,1,0:T(8,128)S(1)}, u32[]{:S(2)}, u32[]{:S(2)}) collective-permute-start(f32[6,8,1024]{2,1,0:T(8,128)S(1)} %get-tuple-element.29), channel_id=1, source_target_pairs={{0,48},{16,32},{32,16},{48,0},{64,112},{80,96},{96,80},{112,64},{1... | collective-permute-start | bytes 589832 | tf_op jit(solution)/shard_map/ppermute | solution.py:205
  36.1 11.3 %collective-permute-start.5 = (f32[6,8,1024]{2,1,0:T(8,128)S(1)}, f32[6,8,1024]{2,1,0:T(8,128)S(1)}, u32[]{:S(2)}, u32[]{:S(2)}) collective-permute-start(f32[6,8,1024]{2,1,0:T(8,128)S(1)} %get-tuple-element.32), channel_id=1, source_target_pairs={{0,96},{16,112},{32,64},{48,80},{64,32},{80,48},{96,0},{112,16},{1... | collective-permute-start | bytes 589832 | tf_op jit(solution)/shard_map/ppermute | solution.py:205
  38.7 11.0 %collective-permute-start.6 = (f32[6,8,1024]{2,1,0:T(8,128)S(1)}, f32[6,8,1024]{2,1,0:T(8,128)S(1)}, u32[]{:S(2)}, u32[]{:S(2)}) collective-permute-start(f32[6,8,1024]{2,1,0:T(8,128)S(1)} %get-tuple-element.33), channel_id=1, source_target_pairs={{0,112},{16,96},{32,80},{48,64},{64,48},{80,32},{96,16},{112,0},{1... | collective-permute-start | bytes 589832 | tf_op jit(solution)/shard_map/ppermute | solution.py:205
  41.2 21.5 %copy-start.5 = (s32[4]{0:T(128)S(1)}, s32[4]{0:T(128)}, u32[]{:S(2)}) copy-start(s32[4]{0:T(128)} %param.11) | copy-start | bytes 52
  41.2 19.3 %collective-permute-start.7 = (f32[6,8,1024]{2,1,0:T(8,128)S(1)}, f32[6,8,1024]{2,1,0:T(8,128)S(1)}, u32[]{:S(2)}, u32[]{:S(2)}) collective-permute-start(f32[6,8,1024]{2,1,0:T(8,128)S(1)} %get-tuple-element.34), channel_id=1, source_target_pairs={{0,128},{16,144},{32,160},{48,176},{64,192},{80,208},{96,224},{112... | collective-permute-start | bytes 589832 | tf_op jit(solution)/shard_map/ppermute | solution.py:205
  42.6 29.1 %copy-start.2 = (f32[4,8,1024]{2,1,0:T(8,128)S(1)}, f32[4,8,1024]{2,1,0:T(8,128)}, u32[]{:S(2)}) copy-start(f32[4,8,1024]{2,1,0:T(8,128)} %param.13) | copy-start | bytes 393220
  42.6 29.1 %copy-start.3 = (s32[4,8,1024]{2,1,0:T(8,128)S(1)}, s32[4,8,1024]{2,1,0:T(8,128)}, u32[]{:S(2)}) copy-start(s32[4,8,1024]{2,1,0:T(8,128)} %param.10) | copy-start | bytes 393220
  42.6 29.3 %copy-start.4 = (f32[4,8,6]{1,0,2:T(4,128)S(1)}, f32[4,8,6]{1,0,2:T(4,128)}, u32[]{:S(2)}) copy-start(f32[4,8,6]{1,0,2:T(4,128)} %param.12) | copy-start | bytes 2308
  42.7 20.0 %collective-permute-start.8 = (f32[6,8,1024]{2,1,0:T(8,128)S(1)}, f32[6,8,1024]{2,1,0:T(8,128)S(1)}, u32[]{:S(2)}, u32[]{:S(2)}) collective-permute-start(f32[6,8,1024]{2,1,0:T(8,128)S(1)} %get-tuple-element.35), channel_id=1, source_target_pairs={{0,144},{16,128},{32,176},{48,160},{64,208},{80,192},{96,240},{112... | collective-permute-start | bytes 589832 | tf_op jit(solution)/shard_map/ppermute | solution.py:205
  45.5 17.2 %collective-permute-start.9 = (f32[6,8,1024]{2,1,0:T(8,128)S(1)}, f32[6,8,1024]{2,1,0:T(8,128)S(1)}, u32[]{:S(2)}, u32[]{:S(2)}) collective-permute-start(f32[6,8,1024]{2,1,0:T(8,128)S(1)} %get-tuple-element.36), channel_id=1, source_target_pairs={{0,160},{16,176},{32,128},{48,144},{64,224},{80,240},{96,192},{112... | collective-permute-start | bytes 589832 | tf_op jit(solution)/shard_map/ppermute | solution.py:205
  47.4 15.3 %collective-permute-start = (f32[6,8,1024]{2,1,0:T(8,128)S(1)}, f32[6,8,1024]{2,1,0:T(8,128)S(1)}, u32[]{:S(2)}, u32[]{:S(2)}) collective-permute-start(f32[6,8,1024]{2,1,0:T(8,128)S(1)} %get-tuple-element.27), channel_id=1, source_target_pairs={{0,16},{16,0},{32,48},{48,32},{64,80},{80,64},{96,112},{112,96},{1... | collective-permute-start | bytes 589832 | tf_op jit(solution)/shard_map/ppermute | solution.py:205
  49.8 18.8 %collective-permute-start.3 = (f32[6,8,1024]{2,1,0:T(8,128)S(1)}, f32[6,8,1024]{2,1,0:T(8,128)S(1)}, u32[]{:S(2)}, u32[]{:S(2)}) collective-permute-start(f32[6,8,1024]{2,1,0:T(8,128)S(1)} %get-tuple-element.30), channel_id=1, source_target_pairs={{0,64},{16,80},{32,96},{48,112},{64,0},{80,16},{96,32},{112,48},{1... | collective-permute-start | bytes 589832 | tf_op jit(solution)/shard_map/ppermute | solution.py:205
  60.5 8.0 %collective-permute-start.4 = (f32[6,8,1024]{2,1,0:T(8,128)S(1)}, f32[6,8,1024]{2,1,0:T(8,128)S(1)}, u32[]{:S(2)}, u32[]{:S(2)}) collective-permute-start(f32[6,8,1024]{2,1,0:T(8,128)S(1)} %get-tuple-element.31), channel_id=1, source_target_pairs={{0,80},{16,64},{32,112},{48,96},{64,16},{80,0},{96,48},{112,32},{1... | collective-permute-start | bytes 589832 | tf_op jit(solution)/shard_map/ppermute | solution.py:205
  68.8 7.0 %collective-permute-start.15 = (f32[6,8,1024]{2,1,0:T(8,128)S(1)}, f32[6,8,1024]{2,1,0:T(8,128)S(1)}, u32[]{:S(2)}, u32[]{:S(2)}) collective-permute-start(f32[6,8,1024]{2,1,0:T(8,128)S(1)} %add_add_fusion), channel_id=1, source_target_pairs={{0,0},{1,16},{2,32},{3,48},{4,64},{5,80},{6,96},{7,112},{8,128},{9... | collective-permute-start | bytes 589832 | tf_op jit(solution)/shard_map/ppermute | solution.py:207
  77.1 36.0 %all-to-all-start = ((f32[16,8,128]{2,1,0:T(8,128)}), f32[16,8,128]{2,1,0:T(8,128)S(1)}, u32[]{:S(2)}, u32[]{:S(2)}) async-start(f32[16,8,128]{2,1,0:T(8,128)} %get-tuple-element.43), calls=%async_computation | async-start | bytes 131072 | tf_op jit(solution)/shard_map/all_to_all | solution.py:223
  114.3 11.1 %all-to-all-start.1 = ((f32[16,8,128]{2,1,0:T(8,128)}), f32[16,8,128]{2,1,0:T(8,128)S(1)}, u32[]{:S(2)}, u32[]{:S(2)}) async-start(f32[16,8,128]{2,1,0:T(8,128)} %get-tuple-element.46), calls=%async_computation.1 | async-start | bytes 131072 | tf_op jit(solution)/shard_map/all_to_all | solution.py:223
